TPU v7x, 8 devices: a whole 2x2x1 slice. The times are simulated.
8 devices in a mesh: dp: 1 (over z), tp: 8 (over y, x, core).
Axes of the slice: x: 2, y: 2, z: 1, core: 2. Of those that a mesh axis runs over, the one named last changes fastest.
Arguments:
- hidden_in: bfloat16 [12, 768, 1024], P('dp', 'tp')
- ln1_gain: bfloat16 [1024], replicated
- ln1_bias: bfloat16 [1024], replicated
- w_q: bfloat16 [1024, 1024], P(None, 'tp')
- b_q: bfloat16 [1024], P('tp')
- w_k: bfloat16 [1024, 1024], P(None, 'tp')
- w_v: bfloat16 [1024, 1024], P(None, 'tp')
- b_v: bfloat16 [1024], P('tp')
- w_o: bfloat16 [1024, 1024], P('tp')
- b_o: bfloat16 [1024], replicated
- ln2_gain: bfloat16 [1024], replicated
- ln2_bias: bfloat16 [1024], replicated
- w_fc1: bfloat16 [1024, 4096], P(None, 'tp')
- b_fc1: bfloat16 [4096], P('tp')
- w_fc2: bfloat16 [4096, 1024], P('tp')
- b_fc2: bfloat16 [1024], replicated
- post_gain: bfloat16 [1024], replicated
- post_bias: bfloat16 [1024], replicated
- w_ck: bfloat16 [2, 1024, 1024], P(None, None, 'tp')
- w_cv: bfloat16 [2, 1024, 1024], P(None, None, 'tp')
- b_cv: bfloat16 [2, 1024], P(None, 'tp')
Outputs:
- output 1: bfloat16 [12, 768, 1024], P('dp', 'tp')
- output 2: bfloat16 [2, 12, 768, 16, 64], P(None, 'dp', None, 'tp')
- output 3: bfloat16 [2, 12, 768, 16, 64], P(None, 'dp', None, 'tp')
All inputs are finite; a program needn't handle non-finite values.
Results may differ from a plain program's by a relative error of at most 0.0160126.
Values are sent between devices in bfloat16 or wider.
A program may use at most 1 GiB of HBM per device.

v0:
```python
import functools

import jax
import jax.numpy as jnp
from jax import lax
from jax.experimental import pallas as pl
from jax.experimental.pallas import tpu as pltpu
from jax.sharding import PartitionSpec as P

HEAD_DIM = 64
ATTN_SCALE = HEAD_DIM ** -0.25
LN_EPS = 1e-5
CLIPS = 12
PER_CHIP = 3
FR = 96
HALF = 4 * FR
FRAMES = 8 * FR
D = 1024
LOC = 128
HID = 512
NQ = 4 * LOC
NH = 4 * HID
QROWS = 256
F32, BF16 = jnp.float32, jnp.bfloat16


def ln_rows(values, gain, bias):
    centered = values - jnp.mean(values, axis=-1, keepdims=True)
    row_var = jnp.mean(centered * centered, axis=-1, keepdims=True)
    return (centered * lax.rsqrt(row_var + LN_EPS) * gain + bias).astype(BF16)


def kernel(hid, wq_h, wk_h, wv_h, wo_h, w1_h, w2_h, ck_h, cv_h,
           bq_v, bv_v, b1_v, bcv_v, ln1g, ln1b, ln2g, ln2b, postg, postb, bo_v, bfc2,
           enc_o, kc_o, vc_o,
           xb, am, ex_s, ex_r, wqkv, wo, w1, w2, bias, qkv, kz, vz, ob, g, acc, wct, bct, ea,
           x_r, x_s, w_r, w_s, b_r, b_s, am_r, am_s, ex_rs, ex_ss, ex_x, ex_y, ex_d, ex_f, es_x, es_y, es_d, es_f, c_s, free):
    t = lax.axis_index("tp")
    c, k = t // 2, t % 2
    cx, cy = c % 2, c // 2
    cxn = 2 * cy + (1 - cx)
    cyn = 2 * (1 - cy) + cx
    cdg = 2 * (1 - cy) + (1 - cx)
    ks = 1 - k
    sib, xn, yn, dg = 2 * c + ks, 2 * cxn + k, 2 * cyn + k, 2 * cdg + k

    def remote(src, dst, ssem, rsem, dev):
        return pltpu.make_async_remote_copy(src_ref=src, dst_ref=dst, send_sem=ssem, recv_sem=rsem,
                                            device_id={"tp": dev}, device_id_type=pl.DeviceIdType.MESH)

    def wait_recv(ref, rsem):
        pltpu.make_async_copy(ref, ref, rsem).wait()

    def row(ref):
        return ref[...].astype(F32).reshape(1, ref.shape[0])

    bias[c, 0:1, :] = row(bq_v)
    bias[c, 1:2, :] = row(bv_v)
    b1_row = row(b1_v)
    for q in range(4):
        bias[c, 2 + q:3 + q, :] = b1_row[:, q * LOC:(q + 1) * LOC]
    for l in range(2):
        bct[l] = jnp.transpose(jnp.broadcast_to(bcv_v[l:l + 1, :].astype(F32), (LOC, LOC)))

    barrier = pltpu.get_barrier_semaphore()
    for peer in (sib, xn, yn, dg):
        pl.semaphore_signal(barrier, inc=1, device_id={"tp": peer}, device_id_type=pl.DeviceIdType.MESH)
    pl.semaphore_wait(barrier, 4)

    def xslot(chip, late):
        return xb.at[pl.ds(2, 1) if late else pl.ds(0, 2), pl.ds(chip * FR, FR), :]

    def xsource(chip, late):
        return hid.at[pl.ds(chip * PER_CHIP + 2, 1) if late else pl.ds(chip * PER_CHIP, 2)]

    def wfull(i, chip):
        if i < 3:
            return wqkv.at[i, :, pl.ds(pl.multiple_of(chip * LOC, LOC), LOC)]
        if i == 3:
            return wo.at[pl.ds(chip * LOC, LOC)]
        if i == 4:
            return w1.at[:, pl.ds(pl.multiple_of(chip * HID, HID), HID)]
        return w2.at[pl.ds(chip * HID, HID)]

    def whalf(i, chip, hf):
        if i < 3:
            return wqkv.at[i, pl.ds(hf * (D // 2), D // 2), pl.ds(pl.multiple_of(chip * LOC, LOC), LOC)]
        if i == 3:
            return wo.at[pl.ds(chip * LOC + hf * (LOC // 2), LOC // 2)]
        if i == 4:
            return w1.at[pl.ds(hf * (D // 2), D // 2), pl.ds(pl.multiple_of(chip * HID, HID), HID)]
        return w2.at[pl.ds(chip * HID + hf * (HID // 2), HID // 2)]

    w_hbm = (wq_h, wk_h, wv_h, wo_h, w1_h, w2_h)
    sends = []

    def go(src, dst, ssem, rsem, dev):
        cp = remote(src, dst, ssem, rsem, dev)
        cp.start()
        sends.append(cp)

    def send_direct(i):
        go(w_hbm[i], wfull(i, c), w_s.at[i, 0], w_r.at[i, 1], xn)
        go(w_hbm[i], wfull(i, c), w_s.at[i, 1], w_r.at[i, 2], yn)

    def relay(i):
        wait_recv(wfull(i, cxn), w_r.at[i, 1])
        go(whalf(i, cxn, 0), whalf(i, cxn, 0), w_s.at[i, 2], w_r.at[i, 3], yn)
        wait_recv(wfull(i, cyn), w_r.at[i, 2])
        go(whalf(i, cyn, 1), whalf(i, cyn, 1), w_s.at[i, 3], w_r.at[i, 4], xn)

    def wait_rest(i):
        wait_recv(wfull(i, c), w_r.at[i, 0])
        wait_recv(whalf(i, cdg, 0), w_r.at[i, 3])
        wait_recv(whalf(i, cdg, 1), w_r.at[i, 4])

    def send_x(late):
        for r, (dev, chip) in ((2, (dg, cdg)), (0, (xn, cxn)), (1, (yn, cyn))):
            go(xsource(chip, late), xslot(c, late), x_s.at[late, r], x_r.at[late, 1 + r], dev)

    def ln1_stage(j):
        def body(b, _):
            vals = xb[j, pl.ds(b * FR, FR), :].astype(F32)
            am[j, k, b] = ln_rows(vals, row(ln1g), row(ln1b))
            return 0
        lax.fori_loop(0, 4, body, 0)
        cp = remote(am.at[j, k], am.at[j, k], am_s.at[0, j], am_r.at[0, j], sib)
        cp.start()
        a_sends.append(cp)

    def wait_x(late):
        for r, chip in ((0, c), (1, cxn), (2, cyn), (3, cdg)):
            wait_recv(xslot(chip, late), x_r.at[late, r])

    for r, dev in enumerate((xn, yn, dg)):
        go(bias.at[c], bias.at[c], b_s.at[r], b_r.at[r], dev)
    send_x(0)
    for i in range(3):
        send_direct(i)
    for late in range(2):
        pltpu.make_async_copy(xsource(c, late), xslot(c, late), x_r.at[late, 0]).start()
    wc_copies = []
    for i, src in enumerate((ck_h.at[0], ck_h.at[1], cv_h.at[0], cv_h.at[1])):
        cp = pltpu.make_async_copy(src, wct.at[i], c_s.at[i])
        cp.start()
        wc_copies.append(cp)
    for i in range(6):
        pltpu.make_async_copy(w_hbm[i], wfull(i, c), w_r.at[i, 0]).start()

    a_sends = []
    wait_x(0)
    for j in range(2):
        ln1_stage(j)
    send_direct(3)
    for cp in wc_copies:
        cp.wait()
    for r, chip in enumerate((cxn, cyn, cdg)):
        wait_recv(bias.at[chip], b_r.at[r])
    for i in range(4):
        relay(i)
    send_direct(4)
    send_direct(5)
    for i in range(3):
        wait_rest(i)

    def row_of(r):
        return jnp.concatenate([bias[n, r:r + 1, :] for n in range(4)], axis=1)

    lane = lax.broadcasted_iota(jnp.int32, (FRAMES, LOC), 1)

    def attention_stage(j):
        wait_recv(am.at[j, ks], am_r.at[0, j])
        bq, bv = row_of(0), row_of(1)

        def project(r, _):
            rows = pl.ds(r * HALF, HALF)
            a = am[j, r].reshape(HALF, D)
            qkv[0, rows, :] = ((jnp.dot(a, wqkv[0], preferred_element_type=F32) + bq) * ATTN_SCALE).astype(BF16)
            qkv[1, rows, :] = (jnp.dot(a, wqkv[1], preferred_element_type=F32) * ATTN_SCALE).astype(BF16)
            qkv[2, rows, :] = (jnp.dot(a, wqkv[2], preferred_element_type=F32) + bv).astype(BF16)
            return 0
        lax.fori_loop(0, 2, project, 0)

        def pair(p, _):
            cols = pl.ds(pl.multiple_of(p * LOC, LOC), LOC)
            kp, vp = qkv[1, :, cols], qkv[2, :, cols]
            zero = jnp.zeros_like(kp)
            kz[0] = jnp.where(lane < HEAD_DIM, kp, zero)
            kz[1] = jnp.where(lane < HEAD_DIM, zero, kp)
            vz[0] = jnp.where(lane < HEAD_DIM, vp, zero)
            vz[1] = jnp.where(lane < HEAD_DIM, zero, vp)

            def attend(r, _):
                rows = pl.ds(r * QROWS, QROWS)
                qb = qkv[0, rows, cols]
                out = None
                for hh in range(2):
                    s = lax.dot_general(qb, kz[hh], (((1,), (1,)), ((), ())), preferred_element_type=F32)
                    e = jnp.exp(s - jnp.max(s, axis=-1, keepdims=True))
                    prob = (e * (1.0 / jnp.sum(e, axis=-1, keepdims=True))).astype(BF16)
                    part = jnp.dot(prob, vz[hh], preferred_element_type=F32)
                    out = part if out is None else out + part
                ob[rows, cols] = out.astype(BF16)
                return 0
            lax.fori_loop(0, FRAMES // QROWS, attend, 0)
            return 0
        lax.fori_loop(0, 4, pair, 0)

    own = pl.ds(k * HALF, HALF)
    oth = pl.ds(ks * HALF, HALF)

    def swap_partials(phase, j, lhs, weight):
        for n in range(2):
            cols = slice(n * 512, (n + 1) * 512)
            ex_s[j, :, cols] = jnp.dot(lhs[oth, :], weight[:, cols], preferred_element_type=F32).astype(BF16)
        cp = remote(ex_s.at[j], ex_r.at[j], ex_ss.at[phase, j], ex_rs.at[phase, j], sib)
        cp.start()
        for n in range(2):
            cols = slice(n * 512, (n + 1) * 512)
            acc[:, cols] = jnp.dot(lhs[own, :], weight[:, cols], preferred_element_type=F32)
        wait_recv(ex_r.at[j], ex_rs.at[phase, j])
        cp.wait_send()

    m_sends = []

    def output_stage(j):
        swap_partials(0, j, ob, wo)
        a_sends[j].wait_send()

        def body(b, _):
            rows = pl.ds(b * FR, FR)
            out = (acc[rows, :] + ex_r[j, rows, :].astype(F32) + row(bo_v)).astype(BF16)
            h = (xb[j, rows, :].astype(F32) + out.astype(F32)).astype(BF16)
            xb[j, rows, :] = h
            am[j, k, b] = ln_rows(h.astype(F32), row(ln2g), row(ln2b))
            return 0
        lax.fori_loop(0, 4, body, 0)
        cp = remote(am.at[j, k], am.at[j, k], am_s.at[1, j], am_r.at[1, j], sib)
        cp.start()
        m_sends.append(cp)

    def epiece(group, j, core, hf):
        if group == 3:
            return am.at[j, core, pl.ds(2 * hf, 2)]
        return ea.at[3 * group + j, pl.ds(2 * hf, 2), core]

    def mlp_stage(j):
        wait_recv(am.at[j, ks], am_r.at[1, j])
        if j == 0:
            wait_rest(4)

        def up(i, _):
            n, r = i // 2, i % 2
            rows = pl.ds(r * HALF, HALF)
            cols = pl.ds(pl.multiple_of(n * HID, HID), HID)
            b1 = jnp.concatenate([bias[n, 2 + q:3 + q, :] for q in range(4)], axis=1)
            u = jnp.dot(am[j, r].reshape(HALF, D), w1[:, cols], preferred_element_type=F32) + b1
            g[rows, cols] = (0.5 * u * (1.0 + lax.erf(u * (2.0 ** -0.5)))).astype(BF16)
            return 0
        lax.fori_loop(0, 8, up, 0)
        m_sends[j].wait_send()
        for peer in (sib, xn, yn):
            pl.semaphore_signal(free.at[j], inc=1, device_id={"tp": peer}, device_id_type=pl.DeviceIdType.MESH)
        if j == 0:
            wait_rest(5)
        swap_partials(1, j, g, w2)

        def post(b, _):
            rows = pl.ds(b * FR, FR)
            out = (acc[rows, :] + ex_r[j, rows, :].astype(F32) + row(bfc2)).astype(BF16)
            h2 = (xb[j, rows, :].astype(F32) + out.astype(F32)).astype(BF16)
            ea[j, b, k] = ln_rows(h2.astype(F32), row(postg), row(postb))
            return 0
        lax.fori_loop(0, 4, post, 0)
        for hf in range(2):
            go(epiece(0, j, k, hf), epiece(1, j, k, hf), es_x.at[j, hf], ex_x.at[j, hf], xn)
            go(epiece(0, j, k, 1 - hf), epiece(2, j, k, 1 - hf), es_y.at[j, 1 - hf], ex_y.at[j, 1 - hf], yn)
        for hf in range(2):
            go(epiece(0, j, k, hf), epiece(0, j, k, hf), es_f.at[0, j, hf], ex_f.at[0, j, hf], sib)

    def forward(group, j, hf):
        go(epiece(group, j, k, hf), epiece(group, j, k, hf), es_f.at[group, j, hf], ex_f.at[group, j, hf], sib)

    def relay_e(j):
        pl.semaphore_wait(free.at[j], 3)
        wait_recv(epiece(1, j, k, 0), ex_x.at[j, 0])
        go(epiece(1, j, k, 0), epiece(3, j, k, 0), es_d.at[j, 0], ex_d.at[j, 0], yn)
        forward(1, j, 0)
        wait_recv(epiece(2, j, k, 1), ex_y.at[j, 1])
        go(epiece(2, j, k, 1), epiece(3, j, k, 1), es_d.at[j, 1], ex_d.at[j, 1], xn)
        forward(2, j, 1)
        wait_recv(epiece(1, j, k, 1), ex_x.at[j, 1])
        forward(1, j, 1)
        wait_recv(epiece(2, j, k, 0), ex_y.at[j, 0])
        forward(2, j, 0)

    def take_diagonal(j):
        for hf in range(2):
            wait_recv(epiece(3, j, k, hf), ex_d.at[j, hf])
            forward(3, j, hf)

    def write_caches(clip, ec):
        for i in range(4):
            r = lax.dot_general(wct[i], ec, (((0,), (1,)), ((), ())), preferred_element_type=F32)
            if i >= 2:
                r = r + jnp.concatenate([bct[i - 2]] * 6, axis=1)
            (kc_o, vc_o)[i // 2][i % 2, clip] = r.astype(BF16)

    def near_cache(group, j):
        chip = jnp.where(group == 0, c, jnp.where(group == 1, cxn, cyn))
        clip = chip * PER_CHIP + j
        for hf in range(2):
            wait_recv(ea.at[3 * group + j, pl.ds(2 * hf, 2), ks], ex_f.at[group, j, hf])
        enc_o[clip] = ea[3 * group + j, c, k]
        write_caches(clip, ea[3 * group + j].reshape(FRAMES, D))

    def far_cache(j, _):
        clip = cdg * PER_CHIP + j
        for hf in range(2):
            wait_recv(epiece(3, j, ks, hf), ex_f.at[3, j, hf])
        enc_o[clip] = am[j, k, c]
        write_caches(clip, jnp.concatenate([am[j, core, b] for b in range(4) for core in range(2)], axis=0))
        return 0

    attention_stage(0)
    wait_rest(3)
    output_stage(0)
    attention_stage(1)
    relay(4)
    output_stage(1)
    relay(5)
    send_x(1)
    mlp_stage(0)
    mlp_stage(1)
    wait_x(1)
    ln1_stage(2)
    attention_stage(2)
    relay_e(0)
    output_stage(2)
    mlp_stage(2)
    relay_e(1)

    def first(i, _):
        near_cache(jnp.where(i < 3, 0, 1 + (i + 1) % 2), jnp.where(i < 3, i, (i - 3) // 2))
        return 0
    lax.fori_loop(0, 7, first, 0)
    take_diagonal(0)
    far_cache(0, 0)
    relay_e(2)

    def second(i, _):
        near_cache(1 + i, 2)
        return 0
    lax.fori_loop(0, 2, second, 0)
    take_diagonal(1)
    take_diagonal(2)
    lax.fori_loop(1, 3, far_cache, 0)
    for cp in sends:
        cp.wait_send()


def device_body(hidden_loc, ln1_gain, ln1_bias, w_q, b_q, w_k, w_v, b_v, w_o, b_o, ln2_gain, ln2_bias, w_fc1, b_fc1, w_fc2, b_fc2, post_gain, post_bias, w_ck, w_cv, b_cv):
    anyspec = pl.BlockSpec(memory_space=pl.ANY)
    vspec = pl.BlockSpec(memory_space=pltpu.VMEM)
    dma = pltpu.SemaphoreType.DMA
    cache = pltpu.VMEM((2, CLIPS, LOC, FRAMES), BF16)
    enc, kc, vc = pl.pallas_call(
        kernel,
        out_shape=(pltpu.VMEM((CLIPS, FR, D), BF16), cache, cache),
        in_specs=[anyspec] * 9 + [vspec] * 12,
        out_specs=(vspec, vspec, vspec),
        scratch_shapes=[
            pltpu.VMEM((PER_CHIP, HALF, D), BF16),
            pltpu.VMEM((PER_CHIP, 2, 4, FR, D), BF16),
            pltpu.VMEM((PER_CHIP, HALF, D), BF16),
            pltpu.VMEM((PER_CHIP, HALF, D), BF16),
            pltpu.VMEM((3, D, NQ), BF16),
            pltpu.VMEM((NQ, D), BF16),
            pltpu.VMEM((D, NH), BF16),
            pltpu.VMEM((NH, D), BF16),
            pltpu.VMEM((4, 8, LOC), F32),
            pltpu.VMEM((3, FRAMES, NQ), BF16),
            pltpu.VMEM((2, FRAMES, LOC), BF16),
            pltpu.VMEM((2, FRAMES, LOC), BF16),
            pltpu.VMEM((FRAMES, NQ), BF16),
            pltpu.VMEM((FRAMES, NH), BF16),
            pltpu.VMEM((HALF, D), F32),
            pltpu.VMEM((4, D, LOC), BF16),
            pltpu.VMEM((2, LOC, LOC), F32),
            pltpu.VMEM((9, 4, 2, FR, D), BF16),
            dma((2, 4)), dma((2, 3)), dma((6, 5)), dma((6, 4)), dma((3,)), dma((3,)),
            dma((2, 3)), dma((2, 3)), dma((2, 3)), dma((2, 3)),
            dma((3, 2)), dma((3, 2)), dma((3, 2)), dma((4, 3, 2)),
            dma((3, 2)), dma((3, 2)), dma((3, 2)), dma((4, 3, 2)),
            dma((4,)), pltpu.SemaphoreType.REGULAR((3,)),
        ],
        compiler_params=pltpu.CompilerParams(collective_id=0, has_side_effects=True, vmem_limit_bytes=55000000),
        name="encoder_layer",
    )(hidden_loc, w_q, w_k, w_v, w_o, w_fc1, w_fc2, w_ck, w_cv,
      b_q, b_v, b_fc1, b_cv, ln1_gain, ln1_bias, ln2_gain, ln2_bias, post_gain, post_bias, b_o, b_fc2)

    def heads_last(cached):
        return cached.reshape(2, CLIPS, LOC // HEAD_DIM, HEAD_DIM, FRAMES).transpose(0, 1, 4, 2, 3)
    return enc, heads_last(kc), heads_last(vc)


def solution(mesh):
    in_specs = (P("dp", "tp", None), P(), P(), P(None, "tp"), P("tp"), P(None, "tp"), P(None, "tp"), P("tp"), P("tp", None), P(), P(), P(), P(None, "tp"), P("tp"), P("tp", None), P(), P(), P(), P(None, None, "tp"), P(None, None, "tp"), P(None, "tp"))
    out_specs = (P("dp", "tp", None), P(None, "dp", None, "tp", None), P(None, "dp", None, "tp", None))
    return jax.shard_map(device_body, mesh=mesh, in_specs=in_specs, out_specs=out_specs, check_vma=False)
```

profile of v0, /device:TPU:0, one launch (start us, length us, event | category | flops | bytes accessed | tf_op | source)
XLA Modules:
  0.0 227.2 jit_solution(13891360884485723920)
XLA Ops:
  0.6 220.7 %encoder_layer.1 = (bf16[12,96,1024]{2,1,0:T(8,128)(2,1)S(1)}, bf16[2,12,128,768]{3,2,1,0:T(8,128)(2,1)S(1)}, bf16[2,12,128,768]{3,2,1,0:T(8,128)(2,1)S(1)}) custom-call(bf16[12,96,1024]{2,1,0:T(8,128)(2,1)} %hid.1, bf16[1024,128]{1,0:T(8,128)(2,1)} %wq_h.1, bf16[1024,128]{1,0:T(8,128)(2,1)} %wk_h.1, bf16[1024,128]{1,0:T(8,128)(2,1)} %wv_h.1, ...), custom_call_target="tpu_custom_call" | custom-call | tf_op jit(solution)/shard_map/encoder_layer/pallas_call | solution.py:367
  221.4 1.4 copy.27
  222.8 2.2 copy.28
  225.0 2.2 copy.29
where the time goes:
time: 227 us
  Pallas kernels  221 us (97%)
  local copies, waits for them, and re-layouts  5.78 us (3%)
    pallas_call x1, Pallas kernels, device_body(): pl.pallas_call(kernel, out_shape=(pltpu.VMEM((CLIPS, FR, D), BF16), cache...  221 us
    unnamed x3, local copies, waits for them, and re-layouts  5.78 us

commit v1 on v0

--- a/solution.py
+++ b/solution.py
@@ -32,8 +32,8 @@
 
 def kernel(hid, wq_h, wk_h, wv_h, wo_h, w1_h, w2_h, ck_h, cv_h,
            bq_v, bv_v, b1_v, bcv_v, ln1g, ln1b, ln2g, ln2b, postg, postb, bo_v, bfc2,
-           enc_o, kc_o, vc_o,
-           xb, am, ex_s, ex_r, wqkv, wo, w1, w2, bias, qkv, kz, vz, ob, g, acc, wct, bct, ea,
+           enc_o, kc_o, vc_o, am, wct, bct,
+           xb, ex_s, ex_r, wqkv, wo, w1, w2, bias, qkv, kz, vz, ob, g, acc, wc, ea,
            x_r, x_s, w_r, w_s, b_r, b_s, am_r, am_s, ex_rs, ex_ss, ex_x, ex_y, ex_d, ex_f, es_x, es_y, es_d, es_f, c_s, free):
     t = lax.axis_index("tp")
     c, k = t // 2, t % 2
@@ -141,7 +141,7 @@
         pltpu.make_async_copy(xsource(c, late), xslot(c, late), x_r.at[late, 0]).start()
     wc_copies = []
     for i, src in enumerate((ck_h.at[0], ck_h.at[1], cv_h.at[0], cv_h.at[1])):
-        cp = pltpu.make_async_copy(src, wct.at[i], c_s.at[i])
+        cp = pltpu.make_async_copy(src, wc.at[i], c_s.at[i])
         cp.start()
         wc_copies.append(cp)
     for i in range(6):
@@ -154,6 +154,8 @@
     send_direct(3)
     for cp in wc_copies:
         cp.wait()
+    for i in range(4):
+        wct[i * LOC:(i + 1) * LOC, :] = jnp.transpose(wc[i])
     for r, chip in enumerate((cxn, cyn, cdg)):
         wait_recv(bias.at[chip], b_r.at[r])
     for i in range(4):
@@ -300,11 +302,7 @@
             forward(3, j, hf)
 
     def write_caches(clip, ec):
-        for i in range(4):
-            r = lax.dot_general(wct[i], ec, (((0,), (1,)), ((), ())), preferred_element_type=F32)
-            if i >= 2:
-                r = r + jnp.concatenate([bct[i - 2]] * 6, axis=1)
-            (kc_o, vc_o)[i // 2][i % 2, clip] = r.astype(BF16)
+        cache_rows(clip, ec, wct, bct, kc_o, vc_o)
 
     def near_cache(group, j):
         chip = jnp.where(group == 0, c, jnp.where(group == 1, cxn, cyn))
@@ -314,13 +312,12 @@
         enc_o[clip] = ea[3 * group + j, c, k]
         write_caches(clip, ea[3 * group + j].reshape(FRAMES, D))
 
-    def far_cache(j, _):
+    def far_cache(j):
         clip = cdg * PER_CHIP + j
         for hf in range(2):
             wait_recv(epiece(3, j, ks, hf), ex_f.at[3, j, hf])
         enc_o[clip] = am[j, k, c]
-        write_caches(clip, jnp.concatenate([am[j, core, b] for b in range(4) for core in range(2)], axis=0))
-        return 0
+        write_caches(clip, natural_order(am, j))
 
     attention_stage(0)
     wait_rest(3)
@@ -345,7 +342,7 @@
         return 0
     lax.fori_loop(0, 7, first, 0)
     take_diagonal(0)
-    far_cache(0, 0)
+    far_cache(0)
     relay_e(2)
 
     def second(i, _):
@@ -353,25 +350,79 @@
         return 0
     lax.fori_loop(0, 2, second, 0)
     take_diagonal(1)
+    far_cache(1)
     take_diagonal(2)
-    lax.fori_loop(1, 3, far_cache, 0)
+    for hf in range(2):
+        wait_recv(epiece(3, 2, ks, hf), ex_f.at[3, 2, hf])
     for cp in sends:
         cp.wait_send()
+
+
+def natural_order(am, j):
+    return jnp.concatenate([am[j, core, b] for b in range(4) for core in range(2)], axis=0)
+
+
+def cache_rows(clip, ec, wct, bct, k_ref, v_ref):
+    r = lax.dot_general(wct[...], ec, (((1,), (1,)), ((), ())), preferred_element_type=F32)
+    for i in range(4):
+        part = r[i * LOC:(i + 1) * LOC, :]
+        if i >= 2:
+            part = part + jnp.concatenate([bct[i - 2]] * 6, axis=1)
+        (k_ref, v_ref)[i // 2][i % 2, clip] = part.astype(BF16)
+
+
+def writer(enc_v, kc_v, vc_v, am, wct, bct, enc_o, kc_o, vc_o, kl, vl, sem, last_sem):
+    t = lax.axis_index("tp")
+    c, k = t // 2, t % 2
+    cx, cy = c % 2, c // 2
+    cdg = 2 * (1 - cy) + (1 - cx)
+    last = cdg * PER_CHIP + 2
+
+    def copies(clip):
+        cps = [pltpu.make_async_copy(kc_v.at[l, clip], kc_o.at[l, clip], sem) for l in range(2)]
+        cps += [pltpu.make_async_copy(vc_v.at[l, clip], vc_o.at[l, clip], sem) for l in range(2)]
+        return cps + [pltpu.make_async_copy(enc_v.at[clip], enc_o.at[clip], sem)]
+
+    def start(i, _):
+        for cp in copies(lax.rem(last + 1 + i, CLIPS)):
+            cp.start()
+        return 0
+    lax.fori_loop(0, CLIPS - 1, start, 0)
+    cps = [pltpu.make_async_copy(am.at[2, k, c], enc_o.at[last], last_sem)]
+    cps[0].start()
+    cache_rows(0, natural_order(am, 2), wct, bct, kl, vl)
+    for l in range(2):
+        cps.append(pltpu.make_async_copy(kl.at[l, 0], kc_o.at[l, last], last_sem))
+        cps.append(pltpu.make_async_copy(vl.at[l, 0], vc_o.at[l, last], last_sem))
+    for cp in cps[1:]:
+        cp.start()
+
+    def finish(i, _):
+        for cp in copies(lax.rem(last + 1 + i, CLIPS)):
+            cp.wait()
+        return 0
+    lax.fori_loop(0, CLIPS - 1, finish, 0)
+    for cp in cps:
+        cp.wait()
 
 
 def device_body(hidden_loc, ln1_gain, ln1_bias, w_q, b_q, w_k, w_v, b_v, w_o, b_o, ln2_gain, ln2_bias, w_fc1, b_fc1, w_fc2, b_fc2, post_gain, post_bias, w_ck, w_cv, b_cv):
     anyspec = pl.BlockSpec(memory_space=pl.ANY)
     vspec = pl.BlockSpec(memory_space=pltpu.VMEM)
     dma = pltpu.SemaphoreType.DMA
-    cache = pltpu.VMEM((2, CLIPS, LOC, FRAMES), BF16)
-    enc, kc, vc = pl.pallas_call(
+    cache = (2, CLIPS, LOC, FRAMES)
+    parts = pl.pallas_call(
         kernel,
-        out_shape=(pltpu.VMEM((CLIPS, FR, D), BF16), cache, cache),
+        out_shape=(
+            pltpu.VMEM((CLIPS, FR, D), BF16), pltpu.VMEM(cache, BF16), pltpu.VMEM(cache, BF16),
+            pltpu.VMEM((PER_CHIP, 2, 4, FR, D), BF16),
+            pltpu.VMEM((4 * LOC, D), BF16),
+            pltpu.VMEM((2, LOC, LOC), F32),
+        ),
         in_specs=[anyspec] * 9 + [vspec] * 12,
-        out_specs=(vspec, vspec, vspec),
+        out_specs=(vspec,) * 6,
         scratch_shapes=[
             pltpu.VMEM((PER_CHIP, HALF, D), BF16),
-            pltpu.VMEM((PER_CHIP, 2, 4, FR, D), BF16),
             pltpu.VMEM((PER_CHIP, HALF, D), BF16),
             pltpu.VMEM((PER_CHIP, HALF, D), BF16),
             pltpu.VMEM((3, D, NQ), BF16),
@@ -386,7 +437,6 @@
             pltpu.VMEM((FRAMES, NH), BF16),
             pltpu.VMEM((HALF, D), F32),
             pltpu.VMEM((4, D, LOC), BF16),
-            pltpu.VMEM((2, LOC, LOC), F32),
             pltpu.VMEM((9, 4, 2, FR, D), BF16),
             dma((2, 4)), dma((2, 3)), dma((6, 5)), dma((6, 4)), dma((3,)), dma((3,)),
             dma((2, 3)), dma((2, 3)), dma((2, 3)), dma((2, 3)),
@@ -394,10 +444,20 @@
             dma((3, 2)), dma((3, 2)), dma((3, 2)), dma((4, 3, 2)),
             dma((4,)), pltpu.SemaphoreType.REGULAR((3,)),
         ],
-        compiler_params=pltpu.CompilerParams(collective_id=0, has_side_effects=True, vmem_limit_bytes=55000000),
+        compiler_params=pltpu.CompilerParams(collective_id=0, has_side_effects=True, vmem_limit_bytes=48500000),
         name="encoder_layer",
     )(hidden_loc, w_q, w_k, w_v, w_o, w_fc1, w_fc2, w_ck, w_cv,
       b_q, b_v, b_fc1, b_cv, ln1_gain, ln1_bias, ln2_gain, ln2_bias, post_gain, post_bias, b_o, b_fc2)
+
+    enc, kc, vc = pl.pallas_call(
+        writer,
+        out_shape=(jax.ShapeDtypeStruct((CLIPS, FR, D), BF16), jax.ShapeDtypeStruct(cache, BF16), jax.ShapeDtypeStruct(cache, BF16)),
+        in_specs=[vspec] * 6,
+        out_specs=(anyspec,) * 3,
+        scratch_shapes=[pltpu.VMEM((2, 1, LOC, FRAMES), BF16), pltpu.VMEM((2, 1, LOC, FRAMES), BF16), dma, dma],
+        compiler_params=pltpu.CompilerParams(vmem_limit_bytes=8000000),
+        name="writer",
+    )(*parts)
 
     def heads_last(cached):
         return cached.reshape(2, CLIPS, LOC // HEAD_DIM, HEAD_DIM, FRAMES).transpose(0, 1, 4, 2, 3)

time: 227 us -> 224 us (0.987)
  local copies, waits for them, and re-layouts: 5.78 us -> 0 us
    unnamed x3 -> x0, local copies, waits for them, and re-layouts: 5.78 us -> none
    pallas_call x1 -> x2, Pallas kernels: 221 us -> 223 us  [the longest x1 218 us: device_body(): pl.pallas_call(kernel, out_shape=(pltpu.VMEM((CLIPS, FR, D), BF16), pltpu...]
where the time goes in v1:
time: 224 us; the launch traced here: 223 us
  Pallas kernels  223 us (100%)
    pallas_call x1, Pallas kernels, device_body(): pl.pallas_call(kernel, out_shape=(pltpu.VMEM((CLIPS, FR, D), BF16), pltpu...  218 us

profile of v1, /device:TPU:0, one launch (start us, length us, event | category | flops | bytes accessed | tf_op | source)
XLA Modules:
  0.0 223.4 jit_solution(2067677478524939403)
XLA Ops:
  0.6 218.2 %encoder_layer.1 = (bf16[12,96,1024]{2,1,0:T(8,128)(2,1)S(1)}, bf16[2,12,128,768]{3,2,1,0:T(8,128)(2,1)S(1)}, bf16[2,12,128,768]{3,2,1,0:T(8,128)(2,1)S(1)}, bf1...) custom-call(bf16[12,96,1024]{2,1,0:T(8,128)(2,1)} %hid.1, ...), custom_call_target="tpu_custom_call" | custom-call | tf_op jit(solution)/shard_map/encoder_layer/pallas_call | solution.py:414
  218.9 4.3 %writer.1 = (bf16[12,96,1024]{2,1,0:T(8,128)(2,1)}, bf16[2,12,128,768]{3,2,1,0:T(8,128)(2,1)}, bf16[2,12,128,768]{3,2,1,0:T(8,128)(2,1)}) custom-call(bf16[12,96,1024]{2,1,0:T(8,128)(2,1)S(1)} %get-tuple-element.12.enc_v, bf16[2,12,128,768]{3,2,1,0:T(8,128)(2,1)S(1)} %get-tuple-element.13.kc_v, bf16[2,12,128,768]{3,2,1,0:T(8,128)(2,1)S(1)} %get-tuple-element.14.vc_v, ...), custom_call_target="tpu_custom_call" | custom-call | tf_op jit(solution)/shard_map/writer/pallas_call | solution.py:452

commit v2 on v1

--- a/solution.py
+++ b/solution.py
@@ -33,8 +33,8 @@
 def kernel(hid, wq_h, wk_h, wv_h, wo_h, w1_h, w2_h, ck_h, cv_h,
            bq_v, bv_v, b1_v, bcv_v, ln1g, ln1b, ln2g, ln2b, postg, postb, bo_v, bfc2,
            enc_o, kc_o, vc_o, am, wct, bct,
-           xb, ex_s, ex_r, wqkv, wo, w1, w2, bias, qkv, kz, vz, ob, g, acc, wc, ea,
-           x_r, x_s, w_r, w_s, b_r, b_s, am_r, am_s, ex_rs, ex_ss, ex_x, ex_y, ex_d, ex_f, es_x, es_y, es_d, es_f, c_s, free):
+           xb, xrel, ex_s, ex_r, wqkv, wo, w1, w2, bias, qkv, kz, vz, g, acc, ea,
+           x_r, x_s, xrel_r, w_r, w_s, b_r, b_s, am_r, am_s, ex_rs, ex_ss, ex_x, ex_y, ex_d, ex_f, es_x, es_y, es_d, es_f, c_s, free):
     t = lax.axis_index("tp")
     c, k = t // 2, t % 2
     cx, cy = c % 2, c // 2
@@ -54,21 +54,19 @@
     def row(ref):
         return ref[...].astype(F32).reshape(1, ref.shape[0])
 
-    bias[c, 0:1, :] = row(bq_v)
-    bias[c, 1:2, :] = row(bv_v)
-    b1_row = row(b1_v)
-    for q in range(4):
-        bias[c, 2 + q:3 + q, :] = b1_row[:, q * LOC:(q + 1) * LOC]
-    for l in range(2):
-        bct[l] = jnp.transpose(jnp.broadcast_to(bcv_v[l:l + 1, :].astype(F32), (LOC, LOC)))
-
     barrier = pltpu.get_barrier_semaphore()
     for peer in (sib, xn, yn, dg):
         pl.semaphore_signal(barrier, inc=1, device_id={"tp": peer}, device_id_type=pl.DeviceIdType.MESH)
     pl.semaphore_wait(barrier, 4)
 
+    def xclips(late):
+        return pl.ds(2, 1) if late else pl.ds(0, 2)
+
     def xslot(chip, late):
-        return xb.at[pl.ds(2, 1) if late else pl.ds(0, 2), pl.ds(chip * FR, FR), :]
+        return xb.at[xclips(late), pl.ds(chip * FR, FR), :]
+
+    def xhalf(chip, late, hf):
+        return xb.at[xclips(late), pl.ds(chip * FR + hf * (FR // 2), FR // 2), :]
 
     def xsource(chip, late):
         return hid.at[pl.ds(chip * PER_CHIP + 2, 1) if late else pl.ds(chip * PER_CHIP, 2)]
@@ -100,8 +98,9 @@
         sends.append(cp)
 
     def send_direct(i):
-        go(w_hbm[i], wfull(i, c), w_s.at[i, 0], w_r.at[i, 1], xn)
-        go(w_hbm[i], wfull(i, c), w_s.at[i, 1], w_r.at[i, 2], yn)
+        wait_recv(wfull(i, c), w_r.at[i, 0])
+        go(wfull(i, c), wfull(i, c), w_s.at[i, 0], w_r.at[i, 1], xn)
+        go(wfull(i, c), wfull(i, c), w_s.at[i, 1], w_r.at[i, 2], yn)
 
     def relay(i):
         wait_recv(wfull(i, cxn), w_r.at[i, 1])
@@ -110,13 +109,21 @@
         go(whalf(i, cyn, 1), whalf(i, cyn, 1), w_s.at[i, 3], w_r.at[i, 4], xn)
 
     def wait_rest(i):
-        wait_recv(wfull(i, c), w_r.at[i, 0])
         wait_recv(whalf(i, cdg, 0), w_r.at[i, 3])
         wait_recv(whalf(i, cdg, 1), w_r.at[i, 4])
 
     def send_x(late):
-        for r, (dev, chip) in ((2, (dg, cdg)), (0, (xn, cxn)), (1, (yn, cyn))):
-            go(xsource(chip, late), xslot(c, late), x_s.at[late, r], x_r.at[late, 1 + r], dev)
+        for hf, dev in enumerate((xn, yn)):
+            src = xsource(cdg, late).at[:, pl.ds(hf * (FR // 2), FR // 2), :]
+            go(src, xrel.at[hf, xclips(late)], x_s.at[late, hf], xrel_r.at[late, hf], dev)
+        go(xsource(cxn, late), xslot(c, late), x_s.at[late, 2], x_r.at[late, 1], xn)
+        go(xsource(cyn, late), xslot(c, late), x_s.at[late, 3], x_r.at[late, 2], yn)
+
+    def relay_x(late):
+        for hf, (chip, dev) in enumerate(((cxn, yn), (cyn, xn))):
+            piece = xrel.at[hf, xclips(late)]
+            wait_recv(piece, xrel_r.at[late, hf])
+            go(piece, xhalf(chip, late, hf), x_s.at[late, 4 + hf], x_r.at[late, 3 + hf], dev)
 
     def ln1_stage(j):
         def body(b, _):
@@ -129,23 +136,36 @@
         a_sends.append(cp)
 
     def wait_x(late):
-        for r, chip in ((0, c), (1, cxn), (2, cyn), (3, cdg)):
+        for r, chip in ((0, c), (1, cxn), (2, cyn)):
             wait_recv(xslot(chip, late), x_r.at[late, r])
-
+        for hf in range(2):
+            wait_recv(xhalf(cdg, late, hf), x_r.at[late, 3 + hf])
+
+    send_x(0)
+    for i in range(3):
+        pltpu.make_async_copy(w_hbm[i], wfull(i, c), w_r.at[i, 0]).start()
+    for late in range(2):
+        pltpu.make_async_copy(xsource(c, late), xslot(c, late), x_r.at[late, 0]).start()
+    for i in range(3, 6):
+        pltpu.make_async_copy(w_hbm[i], wfull(i, c), w_r.at[i, 0]).start()
+    wc_copies = []
+    for i, src in enumerate((ck_h.at[0], ck_h.at[1], cv_h.at[0], cv_h.at[1])):
+        for hf in range(2):
+            cp = pltpu.make_async_copy(src.at[pl.ds(hf * 512, 512)], qkv.at[i, pl.ds(0, 512), pl.ds(hf * LOC, LOC)], c_s.at[i, hf])
+            cp.start()
+            wc_copies.append(cp)
+    bias[c, 0:1, :] = row(bq_v)
+    bias[c, 1:2, :] = row(bv_v)
+    b1_row = row(b1_v)
+    for q in range(4):
+        bias[c, 2 + q:3 + q, :] = b1_row[:, q * LOC:(q + 1) * LOC]
+    for l in range(2):
+        bct[l] = jnp.transpose(jnp.broadcast_to(bcv_v[l:l + 1, :].astype(F32), (LOC, LOC)))
+    relay_x(0)
     for r, dev in enumerate((xn, yn, dg)):
         go(bias.at[c], bias.at[c], b_s.at[r], b_r.at[r], dev)
-    send_x(0)
     for i in range(3):
         send_direct(i)
-    for late in range(2):
-        pltpu.make_async_copy(xsource(c, late), xslot(c, late), x_r.at[late, 0]).start()
-    wc_copies = []
-    for i, src in enumerate((ck_h.at[0], ck_h.at[1], cv_h.at[0], cv_h.at[1])):
-        cp = pltpu.make_async_copy(src, wc.at[i], c_s.at[i])
-        cp.start()
-        wc_copies.append(cp)
-    for i in range(6):
-        pltpu.make_async_copy(w_hbm[i], wfull(i, c), w_r.at[i, 0]).start()
 
     a_sends = []
     wait_x(0)
@@ -155,7 +175,8 @@
     for cp in wc_copies:
         cp.wait()
     for i in range(4):
-        wct[i * LOC:(i + 1) * LOC, :] = jnp.transpose(wc[i])
+        for hf in range(2):
+            wct[i * LOC:(i + 1) * LOC, hf * 512:(hf + 1) * 512] = jnp.transpose(qkv[i, 0:512, hf * LOC:(hf + 1) * LOC])
     for r, chip in enumerate((cxn, cyn, cdg)):
         wait_recv(bias.at[chip], b_r.at[r])
     for i in range(4):
@@ -202,7 +223,7 @@
                     prob = (e * (1.0 / jnp.sum(e, axis=-1, keepdims=True))).astype(BF16)
                     part = jnp.dot(prob, vz[hh], preferred_element_type=F32)
                     out = part if out is None else out + part
-                ob[rows, cols] = out.astype(BF16)
+                qkv[3, rows, cols] = out.astype(BF16)
                 return 0
             lax.fori_loop(0, FRAMES // QROWS, attend, 0)
             return 0
@@ -214,19 +235,19 @@
     def swap_partials(phase, j, lhs, weight):
         for n in range(2):
             cols = slice(n * 512, (n + 1) * 512)
-            ex_s[j, :, cols] = jnp.dot(lhs[oth, :], weight[:, cols], preferred_element_type=F32).astype(BF16)
+            ex_s[j, :, cols] = jnp.dot(lhs(oth), weight[:, cols], preferred_element_type=F32).astype(BF16)
         cp = remote(ex_s.at[j], ex_r.at[j], ex_ss.at[phase, j], ex_rs.at[phase, j], sib)
         cp.start()
         for n in range(2):
             cols = slice(n * 512, (n + 1) * 512)
-            acc[:, cols] = jnp.dot(lhs[own, :], weight[:, cols], preferred_element_type=F32)
+            acc[:, cols] = jnp.dot(lhs(own), weight[:, cols], preferred_element_type=F32)
         wait_recv(ex_r.at[j], ex_rs.at[phase, j])
         cp.wait_send()
 
     m_sends = []
 
     def output_stage(j):
-        swap_partials(0, j, ob, wo)
+        swap_partials(0, j, lambda rows: qkv[3, rows, :], wo)
         a_sends[j].wait_send()
 
         def body(b, _):
@@ -246,10 +267,8 @@
             return am.at[j, core, pl.ds(2 * hf, 2)]
         return ea.at[3 * group + j, pl.ds(2 * hf, 2), core]
 
-    def mlp_stage(j):
+    def up_stage(j):
         wait_recv(am.at[j, ks], am_r.at[1, j])
-        if j == 0:
-            wait_rest(4)
 
         def up(i, _):
             n, r = i // 2, i % 2
@@ -257,15 +276,22 @@
             cols = pl.ds(pl.multiple_of(n * HID, HID), HID)
             b1 = jnp.concatenate([bias[n, 2 + q:3 + q, :] for q in range(4)], axis=1)
             u = jnp.dot(am[j, r].reshape(HALF, D), w1[:, cols], preferred_element_type=F32) + b1
-            g[rows, cols] = (0.5 * u * (1.0 + lax.erf(u * (2.0 ** -0.5)))).astype(BF16)
+            act = (0.5 * u * (1.0 + lax.erf(u * (2.0 ** -0.5)))).astype(BF16)
+            if j == 1:
+                qkv[n, rows, :] = act
+            else:
+                g[n, rows, :] = act
             return 0
         lax.fori_loop(0, 8, up, 0)
         m_sends[j].wait_send()
         for peer in (sib, xn, yn):
             pl.semaphore_signal(free.at[j], inc=1, device_id={"tp": peer}, device_id_type=pl.DeviceIdType.MESH)
+
+    def down_stage(j):
+        hidden = qkv if j == 1 else g
+        swap_partials(1, j, lambda rows: jnp.concatenate([hidden[n, rows, :] for n in range(4)], axis=1), w2)
         if j == 0:
-            wait_rest(5)
-        swap_partials(1, j, g, w2)
+            relay_x(1)
 
         def post(b, _):
             rows = pl.ds(b * FR, FR)
@@ -327,14 +353,19 @@
     output_stage(1)
     relay(5)
     send_x(1)
-    mlp_stage(0)
-    mlp_stage(1)
+    wait_rest(4)
+    up_stage(0)
+    up_stage(1)
+    wait_rest(5)
+    down_stage(0)
+    down_stage(1)
     wait_x(1)
     ln1_stage(2)
     attention_stage(2)
     relay_e(0)
     output_stage(2)
-    mlp_stage(2)
+    up_stage(2)
+    down_stage(2)
     relay_e(1)
 
     def first(i, _):
@@ -423,6 +454,7 @@
         out_specs=(vspec,) * 6,
         scratch_shapes=[
             pltpu.VMEM((PER_CHIP, HALF, D), BF16),
+            pltpu.VMEM((2, PER_CHIP, FR // 2, D), BF16),
             pltpu.VMEM((PER_CHIP, HALF, D), BF16),
             pltpu.VMEM((PER_CHIP, HALF, D), BF16),
             pltpu.VMEM((3, D, NQ), BF16),
@@ -430,19 +462,17 @@
             pltpu.VMEM((D, NH), BF16),
             pltpu.VMEM((NH, D), BF16),
             pltpu.VMEM((4, 8, LOC), F32),
-            pltpu.VMEM((3, FRAMES, NQ), BF16),
+            pltpu.VMEM((4, FRAMES, NQ), BF16),
             pltpu.VMEM((2, FRAMES, LOC), BF16),
             pltpu.VMEM((2, FRAMES, LOC), BF16),
-            pltpu.VMEM((FRAMES, NQ), BF16),
-            pltpu.VMEM((FRAMES, NH), BF16),
+            pltpu.VMEM((4, FRAMES, HID), BF16),
             pltpu.VMEM((HALF, D), F32),
-            pltpu.VMEM((4, D, LOC), BF16),
             pltpu.VMEM((9, 4, 2, FR, D), BF16),
-            dma((2, 4)), dma((2, 3)), dma((6, 5)), dma((6, 4)), dma((3,)), dma((3,)),
+            dma((2, 5)), dma((2, 6)), dma((2, 2)), dma((6, 5)), dma((6, 4)), dma((3,)), dma((3,)),
             dma((2, 3)), dma((2, 3)), dma((2, 3)), dma((2, 3)),
             dma((3, 2)), dma((3, 2)), dma((3, 2)), dma((4, 3, 2)),
             dma((3, 2)), dma((3, 2)), dma((3, 2)), dma((4, 3, 2)),
-            dma((4,)), pltpu.SemaphoreType.REGULAR((3,)),
+            dma((4, 2)), pltpu.SemaphoreType.REGULAR((3,)),
         ],
         compiler_params=pltpu.CompilerParams(collective_id=0, has_side_effects=True, vmem_limit_bytes=48500000),
         name="encoder_layer",

time: 224 us -> 219 us (0.978)
  Pallas kernels: 223 us -> 218 us
    pallas_call x1, Pallas kernels: 218 us -> 213 us  [device_body(): pl.pallas_call(kernel, out_shape=(pltpu.VMEM((CLIPS, FR, D), BF16), pltpu...]
where the time goes in v2:
time: 219 us
  Pallas kernels  218 us (100%)
    pallas_call x1, Pallas kernels, device_body(): pl.pallas_call(kernel, out_shape=(pltpu.VMEM((CLIPS, FR, D), BF16), pltpu...  213 us

profile of v2, /device:TPU:0, one launch (start us, length us, event | category | flops | bytes accessed | tf_op | source)
XLA Modules:
  0.0 218.6 jit_solution(13116366232667344940)
XLA Ops:
  0.6 213.5 %encoder_layer.1 = (bf16[12,96,1024]{2,1,0:T(8,128)(2,1)S(1)}, bf16[2,12,128,768]{3,2,1,0:T(8,128)(2,1)S(1)}, bf16[2,12,128,768]{3,2,1,0:T(8,128)(2,1)S(1)}, bf1...) custom-call(bf16[12,96,1024]{2,1,0:T(8,128)(2,1)} %hid.1, ...), custom_call_target="tpu_custom_call" | custom-call | tf_op jit(solution)/shard_map/encoder_layer/pallas_call | solution.py:445
  214.1 4.3 %writer.1 = (bf16[12,96,1024]{2,1,0:T(8,128)(2,1)}, bf16[2,12,128,768]{3,2,1,0:T(8,128)(2,1)}, bf16[2,12,128,768]{3,2,1,0:T(8,128)(2,1)}) custom-call(bf16[12,96,1024]{2,1,0:T(8,128)(2,1)S(1)} %get-tuple-element.12.enc_v, bf16[2,12,128,768]{3,2,1,0:T(8,128)(2,1)S(1)} %get-tuple-element.13.kc_v, bf16[2,12,128,768]{3,2,1,0:T(8,128)(2,1)S(1)} %get-tuple-element.14.vc_v, ...), custom_call_target="tpu_custom_call" | custom-call | tf_op jit(solution)/shard_map/writer/pallas_call | solution.py:482

commit v3 on v2

--- a/solution.py
+++ b/solution.py
@@ -31,10 +31,10 @@
 
 
 def kernel(hid, wq_h, wk_h, wv_h, wo_h, w1_h, w2_h, ck_h, cv_h,
-           bq_v, bv_v, b1_v, bcv_v, ln1g, ln1b, ln2g, ln2b, postg, postb, bo_v, bfc2,
+           bq_h, bv_h, b1_h, bcv_h, ln1g_h, ln1b_h, ln2g_h, ln2b_h, postg_h, postb_h, bo_h, bfc2_h,
            enc_o, kc_o, vc_o, am, wct, bct,
-           xb, xrel, ex_s, ex_r, wqkv, wo, w1, w2, bias, qkv, kz, vz, g, acc, ea,
-           x_r, x_s, xrel_r, w_r, w_s, b_r, b_s, am_r, am_s, ex_rs, ex_ss, ex_x, ex_y, ex_d, ex_f, es_x, es_y, es_d, es_f, c_s, free):
+           bq_v, bv_v, b1_v, bcv_v, ln1g, ln1b, ln2g, ln2b, postg, postb, bo_v, bfc2, xb, xrel, ex_s, ex_r, wqkv, wo, w1, w2, bias, qkv, kz, vz, g, acc, ea,
+           x_r, x_s, xrel_r, w_r, w_s, b_r, b_s, am_r, am_s, ex_rs, ex_ss, ex_x, ex_y, ex_d, ex_f, ex_g, es_x, es_y, es_d, es_f, es_g, c_s, v_s, free):
     t = lax.axis_index("tp")
     c, k = t // 2, t % 2
     cx, cy = c % 2, c // 2
@@ -42,7 +42,7 @@
     cyn = 2 * (1 - cy) + cx
     cdg = 2 * (1 - cy) + (1 - cx)
     ks = 1 - k
-    sib, xn, yn, dg = 2 * c + ks, 2 * cxn + k, 2 * cyn + k, 2 * cdg + k
+    sib, xn, yn = 2 * c + ks, 2 * cxn + k, 2 * cyn + k
 
     def remote(src, dst, ssem, rsem, dev):
         return pltpu.make_async_remote_copy(src_ref=src, dst_ref=dst, send_sem=ssem, recv_sem=rsem,
@@ -55,9 +55,9 @@
         return ref[...].astype(F32).reshape(1, ref.shape[0])
 
     barrier = pltpu.get_barrier_semaphore()
-    for peer in (sib, xn, yn, dg):
+    for peer in (sib, xn, yn):
         pl.semaphore_signal(barrier, inc=1, device_id={"tp": peer}, device_id_type=pl.DeviceIdType.MESH)
-    pl.semaphore_wait(barrier, 4)
+    pl.semaphore_wait(barrier, 3)
 
     def xclips(late):
         return pl.ds(2, 1) if late else pl.ds(0, 2)
@@ -142,6 +142,11 @@
             wait_recv(xhalf(cdg, late, hf), x_r.at[late, 3 + hf])
 
     send_x(0)
+    vec_copies = [pltpu.make_async_copy(src, dst, v_s.at[i]) for i, (src, dst) in enumerate((
+        (bq_h, bq_v), (bv_h, bv_v), (b1_h, b1_v), (bcv_h, bcv_v), (ln1g_h, ln1g), (ln1b_h, ln1b),
+        (ln2g_h, ln2g), (ln2b_h, ln2b), (postg_h, postg), (postb_h, postb), (bo_h, bo_v), (bfc2_h, bfc2)))]
+    for cp in vec_copies:
+        cp.start()
     for i in range(3):
         pltpu.make_async_copy(w_hbm[i], wfull(i, c), w_r.at[i, 0]).start()
     for late in range(2):
@@ -154,6 +159,8 @@
             cp = pltpu.make_async_copy(src.at[pl.ds(hf * 512, 512)], qkv.at[i, pl.ds(0, 512), pl.ds(hf * LOC, LOC)], c_s.at[i, hf])
             cp.start()
             wc_copies.append(cp)
+    for cp in vec_copies:
+        cp.wait()
     bias[c, 0:1, :] = row(bq_v)
     bias[c, 1:2, :] = row(bv_v)
     b1_row = row(b1_v)
@@ -162,7 +169,7 @@
     for l in range(2):
         bct[l] = jnp.transpose(jnp.broadcast_to(bcv_v[l:l + 1, :].astype(F32), (LOC, LOC)))
     relay_x(0)
-    for r, dev in enumerate((xn, yn, dg)):
+    for r, dev in enumerate((xn, yn)):
         go(bias.at[c], bias.at[c], b_s.at[r], b_r.at[r], dev)
     for i in range(3):
         send_direct(i)
@@ -179,6 +186,8 @@
             wct[i * LOC:(i + 1) * LOC, hf * 512:(hf + 1) * 512] = jnp.transpose(qkv[i, 0:512, hf * LOC:(hf + 1) * LOC])
     for r, chip in enumerate((cxn, cyn, cdg)):
         wait_recv(bias.at[chip], b_r.at[r])
+        if r == 0:
+            go(bias.at[cxn], bias.at[cxn], b_s.at[2], b_r.at[2], yn)
     for i in range(4):
         relay(i)
     send_direct(4)
@@ -263,8 +272,6 @@
         m_sends.append(cp)
 
     def epiece(group, j, core, hf):
-        if group == 3:
-            return am.at[j, core, pl.ds(2 * hf, 2)]
         return ea.at[3 * group + j, pl.ds(2 * hf, 2), core]
 
     def up_stage(j):
@@ -312,10 +319,12 @@
     def relay_e(j):
         pl.semaphore_wait(free.at[j], 3)
         wait_recv(epiece(1, j, k, 0), ex_x.at[j, 0])
-        go(epiece(1, j, k, 0), epiece(3, j, k, 0), es_d.at[j, 0], ex_d.at[j, 0], yn)
+        for b in range(2):
+            go(ea.at[PER_CHIP + j, b, k], am.at[j, k, b], es_d.at[j, b], ex_d.at[j, b], yn)
         forward(1, j, 0)
         wait_recv(epiece(2, j, k, 1), ex_y.at[j, 1])
-        go(epiece(2, j, k, 1), epiece(3, j, k, 1), es_d.at[j, 1], ex_d.at[j, 1], xn)
+        for b in range(2, 4):
+            go(ea.at[2 * PER_CHIP + j, b, k], am.at[j, k, b], es_d.at[j, b], ex_d.at[j, b], xn)
         forward(2, j, 1)
         wait_recv(epiece(1, j, k, 1), ex_x.at[j, 1])
         forward(1, j, 1)
@@ -323,9 +332,14 @@
         forward(2, j, 0)
 
     def take_diagonal(j):
-        for hf in range(2):
-            wait_recv(epiece(3, j, k, hf), ex_d.at[j, hf])
-            forward(3, j, hf)
+        for b in (0, 2, 1, 3):
+            piece = am.at[j, k, b]
+            wait_recv(piece, ex_d.at[j, b])
+            go(piece, piece, es_g.at[j, b], ex_g.at[j, b], sib)
+
+    def wait_diagonal(j):
+        for b in range(4):
+            wait_recv(am.at[j, ks, b], ex_g.at[j, b])
 
     def write_caches(clip, ec):
         cache_rows(clip, ec, wct, bct, kc_o, vc_o)
@@ -340,8 +354,7 @@
 
     def far_cache(j):
         clip = cdg * PER_CHIP + j
-        for hf in range(2):
-            wait_recv(epiece(3, j, ks, hf), ex_f.at[3, j, hf])
+        wait_diagonal(j)
         enc_o[clip] = am[j, k, c]
         write_caches(clip, natural_order(am, j))
 
@@ -383,8 +396,7 @@
     take_diagonal(1)
     far_cache(1)
     take_diagonal(2)
-    for hf in range(2):
-        wait_recv(epiece(3, 2, ks, hf), ex_f.at[3, 2, hf])
+    wait_diagonal(2)
     for cp in sends:
         cp.wait_send()
 
@@ -450,9 +462,11 @@
             pltpu.VMEM((4 * LOC, D), BF16),
             pltpu.VMEM((2, LOC, LOC), F32),
         ),
-        in_specs=[anyspec] * 9 + [vspec] * 12,
+        in_specs=[anyspec] * 21,
         out_specs=(vspec,) * 6,
         scratch_shapes=[
+            pltpu.VMEM((LOC,), BF16), pltpu.VMEM((LOC,), BF16), pltpu.VMEM((HID,), BF16), pltpu.VMEM((2, LOC), BF16),
+            *([pltpu.VMEM((D,), BF16)] * 8),
             pltpu.VMEM((PER_CHIP, HALF, D), BF16),
             pltpu.VMEM((2, PER_CHIP, FR // 2, D), BF16),
             pltpu.VMEM((PER_CHIP, HALF, D), BF16),
@@ -470,9 +484,9 @@
             pltpu.VMEM((9, 4, 2, FR, D), BF16),
             dma((2, 5)), dma((2, 6)), dma((2, 2)), dma((6, 5)), dma((6, 4)), dma((3,)), dma((3,)),
             dma((2, 3)), dma((2, 3)), dma((2, 3)), dma((2, 3)),
-            dma((3, 2)), dma((3, 2)), dma((3, 2)), dma((4, 3, 2)),
-            dma((3, 2)), dma((3, 2)), dma((3, 2)), dma((4, 3, 2)),
-            dma((4, 2)), pltpu.SemaphoreType.REGULAR((3,)),
+            dma((3, 2)), dma((3, 2)), dma((3, 4)), dma((3, 3, 2)), dma((3, 4)),
+            dma((3, 2)), dma((3, 2)), dma((3, 4)), dma((3, 3, 2)), dma((3, 4)),
+            dma((4, 2)), dma((12,)), pltpu.SemaphoreType.REGULAR((3,)),
         ],
         compiler_params=pltpu.CompilerParams(collective_id=0, has_side_effects=True, vmem_limit_bytes=48500000),
         name="encoder_layer",

time: 219 us -> 219 us (level)
  no operation moved by 1% of the time
where the time goes in v3:
time: 219 us
  Pallas kernels  218 us (100%)
    pallas_call x1, Pallas kernels, device_body(): pl.pallas_call(kernel, out_shape=(pltpu.VMEM((CLIPS, FR, D), BF16), pltpu...  213 us

profile of v3, /device:TPU:0, one launch (start us, length us, event | category | flops | bytes accessed | tf_op | source)
XLA Modules:
  0.0 218.6 jit_solution(7029503112490606694)
XLA Ops:
  0.6 213.4 %encoder_layer.1 = (bf16[12,96,1024]{2,1,0:T(8,128)(2,1)S(1)}, bf16[2,12,128,768]{3,2,1,0:T(8,128)(2,1)S(1)}, bf16[2,12,128,768]{3,2,1,0:T(8,128)(2,1)S(1)}, bf1...) custom-call(bf16[12,96,1024]{2,1,0:T(8,128)(2,1)} %hid.1, ...), custom_call_target="tpu_custom_call" | custom-call | tf_op jit(solution)/shard_map/encoder_layer/pallas_call | solution.py:457
  214.1 4.3 %writer.1 = (bf16[12,96,1024]{2,1,0:T(8,128)(2,1)}, bf16[2,12,128,768]{3,2,1,0:T(8,128)(2,1)}, bf16[2,12,128,768]{3,2,1,0:T(8,128)(2,1)}) custom-call(bf16[12,96,1024]{2,1,0:T(8,128)(2,1)S(1)} %get-tuple-element.12.enc_v, bf16[2,12,128,768]{3,2,1,0:T(8,128)(2,1)S(1)} %get-tuple-element.13.kc_v, bf16[2,12,128,768]{3,2,1,0:T(8,128)(2,1)S(1)} %get-tuple-element.14.vc_v, ...), custom_call_target="tpu_custom_call" | custom-call | tf_op jit(solution)/shard_map/writer/pallas_call | solution.py:496

commit v4 on v3

--- a/solution.py
+++ b/solution.py
@@ -102,13 +102,23 @@
         go(wfull(i, c), wfull(i, c), w_s.at[i, 0], w_r.at[i, 1], xn)
         go(wfull(i, c), wfull(i, c), w_s.at[i, 1], w_r.at[i, 2], yn)
 
+    def send_halves(i, part):
+        if part == 0:
+            wait_recv(wfull(i, c), w_r.at[i, 0])
+        mine_x, mine_y = whalf(i, c, part), whalf(i, c, 1 - part)
+        go(mine_x, mine_x, w_s.at[i, 4 * part], w_r.at[i, 1 + 4 * part], xn)
+        go(mine_y, mine_y, w_s.at[i, 4 * part + 1], w_r.at[i, 2 + 4 * part], yn)
+
     def relay(i):
-        wait_recv(wfull(i, cxn), w_r.at[i, 1])
+        wait_recv(wfull(i, cxn) if i < 4 else whalf(i, cxn, 0), w_r.at[i, 1])
         go(whalf(i, cxn, 0), whalf(i, cxn, 0), w_s.at[i, 2], w_r.at[i, 3], yn)
-        wait_recv(wfull(i, cyn), w_r.at[i, 2])
+        wait_recv(wfull(i, cyn) if i < 4 else whalf(i, cyn, 1), w_r.at[i, 2])
         go(whalf(i, cyn, 1), whalf(i, cyn, 1), w_s.at[i, 3], w_r.at[i, 4], xn)
 
     def wait_rest(i):
+        if i >= 4:
+            wait_recv(whalf(i, cxn, 1), w_r.at[i, 5])
+            wait_recv(whalf(i, cyn, 0), w_r.at[i, 6])
         wait_recv(whalf(i, cdg, 0), w_r.at[i, 3])
         wait_recv(whalf(i, cdg, 1), w_r.at[i, 4])
 
@@ -168,10 +178,11 @@
         bias[c, 2 + q:3 + q, :] = b1_row[:, q * LOC:(q + 1) * LOC]
     for l in range(2):
         bct[l] = jnp.transpose(jnp.broadcast_to(bcv_v[l:l + 1, :].astype(F32), (LOC, LOC)))
+    send_direct(0)
     relay_x(0)
     for r, dev in enumerate((xn, yn)):
         go(bias.at[c], bias.at[c], b_s.at[r], b_r.at[r], dev)
-    for i in range(3):
+    for i in range(1, 3):
         send_direct(i)
 
     a_sends = []
@@ -188,10 +199,13 @@
         wait_recv(bias.at[chip], b_r.at[r])
         if r == 0:
             go(bias.at[cxn], bias.at[cxn], b_s.at[2], b_r.at[2], yn)
-    for i in range(4):
+    for i in range(3):
         relay(i)
-    send_direct(4)
-    send_direct(5)
+    send_halves(4, 0)
+    relay(3)
+    send_halves(4, 1)
+    send_halves(5, 0)
+    send_halves(5, 1)
     for i in range(3):
         wait_rest(i)
 
@@ -482,7 +496,7 @@
             pltpu.VMEM((4, FRAMES, HID), BF16),
             pltpu.VMEM((HALF, D), F32),
             pltpu.VMEM((9, 4, 2, FR, D), BF16),
-            dma((2, 5)), dma((2, 6)), dma((2, 2)), dma((6, 5)), dma((6, 4)), dma((3,)), dma((3,)),
+            dma((2, 5)), dma((2, 6)), dma((2, 2)), dma((6, 7)), dma((6, 6)), dma((3,)), dma((3,)),
             dma((2, 3)), dma((2, 3)), dma((2, 3)), dma((2, 3)),
             dma((3, 2)), dma((3, 2)), dma((3, 4)), dma((3, 3, 2)), dma((3, 4)),
             dma((3, 2)), dma((3, 2)), dma((3, 4)), dma((3, 3, 2)), dma((3, 4)),

time: 219 us -> 219 us (level)
  no operation moved by 1% of the time
where the time goes in v4:
time: 219 us
  Pallas kernels  218 us (100%)
    pallas_call x1, Pallas kernels, device_body(): pl.pallas_call(kernel, out_shape=(pltpu.VMEM((CLIPS, FR, D), BF16), pltpu...  214 us

profile of v4, /device:TPU:0, one launch (start us, length us, event | category | flops | bytes accessed | tf_op | source)
XLA Modules:
  0.0 218.8 jit_solution(11261521872264921447)
XLA Ops:
  0.6 213.6 %encoder_layer.1 = (bf16[12,96,1024]{2,1,0:T(8,128)(2,1)S(1)}, bf16[2,12,128,768]{3,2,1,0:T(8,128)(2,1)S(1)}, bf16[2,12,128,768]{3,2,1,0:T(8,128)(2,1)S(1)}, bf1...) custom-call(bf16[12,96,1024]{2,1,0:T(8,128)(2,1)} %hid.1, ...), custom_call_target="tpu_custom_call" | custom-call | tf_op jit(solution)/shard_map/encoder_layer/pallas_call | solution.py:471
  214.3 4.3 %writer.1 = (bf16[12,96,1024]{2,1,0:T(8,128)(2,1)}, bf16[2,12,128,768]{3,2,1,0:T(8,128)(2,1)}, bf16[2,12,128,768]{3,2,1,0:T(8,128)(2,1)}) custom-call(bf16[12,96,1024]{2,1,0:T(8,128)(2,1)S(1)} %get-tuple-element.12.enc_v, bf16[2,12,128,768]{3,2,1,0:T(8,128)(2,1)S(1)} %get-tuple-element.13.kc_v, bf16[2,12,128,768]{3,2,1,0:T(8,128)(2,1)S(1)} %get-tuple-element.14.vc_v, ...), custom_call_target="tpu_custom_call" | custom-call | tf_op jit(solution)/shard_map/writer/pallas_call | solution.py:510

commit v5 on v4

--- a/solution.py
+++ b/solution.py
@@ -185,11 +185,12 @@
     for i in range(1, 3):
         send_direct(i)
 
+    send_direct(3)
+    send_halves(4, 0)
     a_sends = []
     wait_x(0)
     for j in range(2):
         ln1_stage(j)
-    send_direct(3)
     for cp in wc_copies:
         cp.wait()
     for i in range(4):
@@ -201,7 +202,6 @@
             go(bias.at[cxn], bias.at[cxn], b_s.at[2], b_r.at[2], yn)
     for i in range(3):
         relay(i)
-    send_halves(4, 0)
     relay(3)
     send_halves(4, 1)
     send_halves(5, 0)

time: 219 us -> 218 us (level)
  no operation moved by 1% of the time
where the time goes in v5:
time: 218 us
  Pallas kernels  217 us (100%)
    pallas_call x1, Pallas kernels, device_body(): pl.pallas_call(kernel, out_shape=(pltpu.VMEM((CLIPS, FR, D), BF16), pltpu...  213 us

profile of v5, /device:TPU:0, one launch (start us, length us, event | category | flops | bytes accessed | tf_op | source)
XLA Modules:
  0.0 217.9 jit_solution(18212161758220125255)
XLA Ops:
  0.6 212.8 %encoder_layer.1 = (bf16[12,96,1024]{2,1,0:T(8,128)(2,1)S(1)}, bf16[2,12,128,768]{3,2,1,0:T(8,128)(2,1)S(1)}, bf16[2,12,128,768]{3,2,1,0:T(8,128)(2,1)S(1)}, bf1...) custom-call(bf16[12,96,1024]{2,1,0:T(8,128)(2,1)} %hid.1, ...), custom_call_target="tpu_custom_call" | custom-call | tf_op jit(solution)/shard_map/encoder_layer/pallas_call | solution.py:471
  213.5 4.3 %writer.1 = (bf16[12,96,1024]{2,1,0:T(8,128)(2,1)}, bf16[2,12,128,768]{3,2,1,0:T(8,128)(2,1)}, bf16[2,12,128,768]{3,2,1,0:T(8,128)(2,1)}) custom-call(bf16[12,96,1024]{2,1,0:T(8,128)(2,1)S(1)} %get-tuple-element.12.enc_v, bf16[2,12,128,768]{3,2,1,0:T(8,128)(2,1)S(1)} %get-tuple-element.13.kc_v, bf16[2,12,128,768]{3,2,1,0:T(8,128)(2,1)S(1)} %get-tuple-element.14.vc_v, ...), custom_call_target="tpu_custom_call" | custom-call | tf_op jit(solution)/shard_map/writer/pallas_call | solution.py:510

commit v6 on v5

--- a/solution.py
+++ b/solution.py
@@ -205,7 +205,6 @@
     relay(3)
     send_halves(4, 1)
     send_halves(5, 0)
-    send_halves(5, 1)
     for i in range(3):
         wait_rest(i)
 
@@ -373,24 +372,25 @@
         write_caches(clip, natural_order(am, j))
 
     attention_stage(0)
+    relay(4)
+    send_halves(5, 1)
     wait_rest(3)
     output_stage(0)
     attention_stage(1)
-    relay(4)
+    relay(5)
     output_stage(1)
-    relay(5)
-    send_x(1)
     wait_rest(4)
     up_stage(0)
     up_stage(1)
+    send_x(1)
     wait_rest(5)
     down_stage(0)
     down_stage(1)
     wait_x(1)
     ln1_stage(2)
     attention_stage(2)
+    output_stage(2)
     relay_e(0)
-    output_stage(2)
     up_stage(2)
     down_stage(2)
     relay_e(1)

time: 218 us -> 219 us (level)
  no operation moved by 1% of the time
where the time goes in v6:
time: 219 us
  Pallas kernels  218 us (100%)
    pallas_call x1, Pallas kernels, device_body(): pl.pallas_call(kernel, out_shape=(pltpu.VMEM((CLIPS, FR, D), BF16), pltpu...  214 us

profile of v6, /device:TPU:0, one launch (start us, length us, event | category | flops | bytes accessed | tf_op | source)
XLA Modules:
  0.0 218.8 jit_solution(14049578840499738544)
XLA Ops:
  0.6 213.6 %encoder_layer.1 = (bf16[12,96,1024]{2,1,0:T(8,128)(2,1)S(1)}, bf16[2,12,128,768]{3,2,1,0:T(8,128)(2,1)S(1)}, bf16[2,12,128,768]{3,2,1,0:T(8,128)(2,1)S(1)}, bf1...) custom-call(bf16[12,96,1024]{2,1,0:T(8,128)(2,1)} %hid.1, ...), custom_call_target="tpu_custom_call" | custom-call | tf_op jit(solution)/shard_map/encoder_layer/pallas_call | solution.py:471
  214.3 4.3 %writer.1 = (bf16[12,96,1024]{2,1,0:T(8,128)(2,1)}, bf16[2,12,128,768]{3,2,1,0:T(8,128)(2,1)}, bf16[2,12,128,768]{3,2,1,0:T(8,128)(2,1)}) custom-call(bf16[12,96,1024]{2,1,0:T(8,128)(2,1)S(1)} %get-tuple-element.12.enc_v, bf16[2,12,128,768]{3,2,1,0:T(8,128)(2,1)S(1)} %get-tuple-element.13.kc_v, bf16[2,12,128,768]{3,2,1,0:T(8,128)(2,1)S(1)} %get-tuple-element.14.vc_v, ...), custom_call_target="tpu_custom_call" | custom-call | tf_op jit(solution)/shard_map/writer/pallas_call | solution.py:510

commit v7 on v5

--- a/solution.py
+++ b/solution.py
@@ -73,20 +73,20 @@
 
     def wfull(i, chip):
         if i < 3:
-            return wqkv.at[i, :, pl.ds(pl.multiple_of(chip * LOC, LOC), LOC)]
+            return wqkv.at[i, chip]
         if i == 3:
             return wo.at[pl.ds(chip * LOC, LOC)]
         if i == 4:
-            return w1.at[:, pl.ds(pl.multiple_of(chip * HID, HID), HID)]
+            return w1.at[chip]
         return w2.at[pl.ds(chip * HID, HID)]
 
     def whalf(i, chip, hf):
         if i < 3:
-            return wqkv.at[i, pl.ds(hf * (D // 2), D // 2), pl.ds(pl.multiple_of(chip * LOC, LOC), LOC)]
+            return wqkv.at[i, chip, pl.ds(hf * (D // 2), D // 2)]
         if i == 3:
             return wo.at[pl.ds(chip * LOC + hf * (LOC // 2), LOC // 2)]
         if i == 4:
-            return w1.at[pl.ds(hf * (D // 2), D // 2), pl.ds(pl.multiple_of(chip * HID, HID), HID)]
+            return w1.at[chip, pl.ds(hf * (D // 2), D // 2)]
         return w2.at[pl.ds(chip * HID + hf * (HID // 2), HID // 2)]
 
     w_hbm = (wq_h, wk_h, wv_h, wo_h, w1_h, w2_h)
@@ -218,12 +218,15 @@
         wait_recv(am.at[j, ks], am_r.at[0, j])
         bq, bv = row_of(0), row_of(1)
 
+        def columns(i):
+            return jnp.concatenate([wqkv[i, n] for n in range(4)], axis=1)
+
         def project(r, _):
             rows = pl.ds(r * HALF, HALF)
             a = am[j, r].reshape(HALF, D)
-            qkv[0, rows, :] = ((jnp.dot(a, wqkv[0], preferred_element_type=F32) + bq) * ATTN_SCALE).astype(BF16)
-            qkv[1, rows, :] = (jnp.dot(a, wqkv[1], preferred_element_type=F32) * ATTN_SCALE).astype(BF16)
-            qkv[2, rows, :] = (jnp.dot(a, wqkv[2], preferred_element_type=F32) + bv).astype(BF16)
+            qkv[0, rows, :] = ((jnp.dot(a, columns(0), preferred_element_type=F32) + bq) * ATTN_SCALE).astype(BF16)
+            qkv[1, rows, :] = (jnp.dot(a, columns(1), preferred_element_type=F32) * ATTN_SCALE).astype(BF16)
+            qkv[2, rows, :] = (jnp.dot(a, columns(2), preferred_element_type=F32) + bv).astype(BF16)
             return 0
         lax.fori_loop(0, 2, project, 0)
 
@@ -294,9 +297,8 @@
         def up(i, _):
             n, r = i // 2, i % 2
             rows = pl.ds(r * HALF, HALF)
-            cols = pl.ds(pl.multiple_of(n * HID, HID), HID)
             b1 = jnp.concatenate([bias[n, 2 + q:3 + q, :] for q in range(4)], axis=1)
-            u = jnp.dot(am[j, r].reshape(HALF, D), w1[:, cols], preferred_element_type=F32) + b1
+            u = jnp.dot(am[j, r].reshape(HALF, D), w1[n], preferred_element_type=F32) + b1
             act = (0.5 * u * (1.0 + lax.erf(u * (2.0 ** -0.5)))).astype(BF16)
             if j == 1:
                 qkv[n, rows, :] = act
@@ -485,9 +487,9 @@
             pltpu.VMEM((2, PER_CHIP, FR // 2, D), BF16),
             pltpu.VMEM((PER_CHIP, HALF, D), BF16),
             pltpu.VMEM((PER_CHIP, HALF, D), BF16),
-            pltpu.VMEM((3, D, NQ), BF16),
+            pltpu.VMEM((3, 4, D, LOC), BF16),
             pltpu.VMEM((NQ, D), BF16),
-            pltpu.VMEM((D, NH), BF16),
+            pltpu.VMEM((4, D, HID), BF16),
             pltpu.VMEM((NH, D), BF16),
             pltpu.VMEM((4, 8, LOC), F32),
             pltpu.VMEM((4, FRAMES, NQ), BF16),

time: 218 us -> 218 us (level)
  no operation moved by 1% of the time
where the time goes in v7:
time: 218 us
  Pallas kernels  217 us (100%)
    pallas_call x1, Pallas kernels, device_body(): pl.pallas_call(kernel, out_shape=(pltpu.VMEM((CLIPS, FR, D), BF16), pltpu...  213 us

profile of v7, /device:TPU:0, one launch (start us, length us, event | category | flops | bytes accessed | tf_op | source)
XLA Modules:
  0.0 217.9 jit_solution(15204850131310351245)
XLA Ops:
  0.6 212.8 %encoder_layer.1 = (bf16[12,96,1024]{2,1,0:T(8,128)(2,1)S(1)}, bf16[2,12,128,768]{3,2,1,0:T(8,128)(2,1)S(1)}, bf16[2,12,128,768]{3,2,1,0:T(8,128)(2,1)S(1)}, bf1...) custom-call(bf16[12,96,1024]{2,1,0:T(8,128)(2,1)} %hid.1, ...), custom_call_target="tpu_custom_call" | custom-call | tf_op jit(solution)/shard_map/encoder_layer/pallas_call | solution.py:473
  213.5 4.3 %writer.1 = (bf16[12,96,1024]{2,1,0:T(8,128)(2,1)}, bf16[2,12,128,768]{3,2,1,0:T(8,128)(2,1)}, bf16[2,12,128,768]{3,2,1,0:T(8,128)(2,1)}) custom-call(bf16[12,96,1024]{2,1,0:T(8,128)(2,1)S(1)} %get-tuple-element.12.enc_v, bf16[2,12,128,768]{3,2,1,0:T(8,128)(2,1)S(1)} %get-tuple-element.13.kc_v, bf16[2,12,128,768]{3,2,1,0:T(8,128)(2,1)S(1)} %get-tuple-element.14.vc_v, ...), custom_call_target="tpu_custom_call" | custom-call | tf_op jit(solution)/shard_map/writer/pallas_call | solution.py:512

commit v8 on v7

--- a/solution.py
+++ b/solution.py
@@ -401,17 +401,17 @@
         near_cache(jnp.where(i < 3, 0, 1 + (i + 1) % 2), jnp.where(i < 3, i, (i - 3) // 2))
         return 0
     lax.fori_loop(0, 7, first, 0)
+    relay_e(2)
     take_diagonal(0)
     far_cache(0)
-    relay_e(2)
 
     def second(i, _):
         near_cache(1 + i, 2)
         return 0
     lax.fori_loop(0, 2, second, 0)
     take_diagonal(1)
+    take_diagonal(2)
     far_cache(1)
-    take_diagonal(2)
     wait_diagonal(2)
     for cp in sends:
         cp.wait_send()

time: 218 us -> 218 us (level)
  no operation moved by 1% of the time
where the time goes in v8:
time: 218 us
  Pallas kernels  217 us (100%)
    pallas_call x1, Pallas kernels, device_body(): pl.pallas_call(kernel, out_shape=(pltpu.VMEM((CLIPS, FR, D), BF16), pltpu...  213 us

profile of v8, /device:TPU:0, one launch (start us, length us, event | category | flops | bytes accessed | tf_op | source)
XLA Modules:
  0.0 217.9 jit_solution(12634777239801086994)
XLA Ops:
  0.6 212.8 %encoder_layer.1 = (bf16[12,96,1024]{2,1,0:T(8,128)(2,1)S(1)}, bf16[2,12,128,768]{3,2,1,0:T(8,128)(2,1)S(1)}, bf16[2,12,128,768]{3,2,1,0:T(8,128)(2,1)S(1)}, bf1...) custom-call(bf16[12,96,1024]{2,1,0:T(8,128)(2,1)} %hid.1, ...), custom_call_target="tpu_custom_call" | custom-call | tf_op jit(solution)/shard_map/encoder_layer/pallas_call | solution.py:473
  213.5 4.3 %writer.1 = (bf16[12,96,1024]{2,1,0:T(8,128)(2,1)}, bf16[2,12,128,768]{3,2,1,0:T(8,128)(2,1)}, bf16[2,12,128,768]{3,2,1,0:T(8,128)(2,1)}) custom-call(bf16[12,96,1024]{2,1,0:T(8,128)(2,1)S(1)} %get-tuple-element.12.enc_v, bf16[2,12,128,768]{3,2,1,0:T(8,128)(2,1)S(1)} %get-tuple-element.13.kc_v, bf16[2,12,128,768]{3,2,1,0:T(8,128)(2,1)S(1)} %get-tuple-element.14.vc_v, ...), custom_call_target="tpu_custom_call" | custom-call | tf_op jit(solution)/shard_map/writer/pallas_call | solution.py:512
